TPU v7x, 32 devices: a whole 2x2x4 slice. The times are simulated.
32 devices in a mesh: batch: 4 (over x, core), lat: 8 (over z, y).
Axes of the slice: x: 2, y: 2, z: 4, core: 2. Of those that a mesh axis runs over, the one named last changes fastest.
Arguments:
- predicted: bfloat16 [4, 73, 192, 1440], P('batch', None, 'lat'), may hold values from -64 to 64
- target: bfloat16 [4, 73, 192, 1440], P('batch', None, 'lat'), may hold values from -128 to 128
- legendre_basis: bfloat16 [192, 96, 720], P(None, ('batch', 'lat')), may hold values from -1 to 1
Outputs:
- spectra: float32 [2, 73, 720], replicated
- channel_loss: float32 [73], replicated
All inputs are finite; a program needn't handle non-finite values.
Results may differ from a plain program's by a relative error of at most 0.0003.
Values may be sent and summed in bfloat16 or wider, within the bound.
No kernel may reach another device: no remote copies, remote signals or barrier semaphores. Data moves between devices by JAX's collectives and lax.ppermute only.
A program may use at most 128 MiB of HBM per device.

v0:
```python
import math
import jax
import jax.numpy as jnp
from jax import lax
from jax.sharding import PartitionSpec as P


def fourier_table(lon_count, order_count):
    lon_ids = jnp.arange(lon_count, dtype=jnp.int32)
    order_ids = jnp.arange(order_count, dtype=jnp.int32)
    product_ids = lon_ids[:, None] * order_ids[None, :] % lon_count
    angles = 2.0 * math.pi / lon_count * product_ids.astype(jnp.float32)
    inv_root = 1.0 / math.sqrt(lon_count)
    return jnp.stack([jnp.cos(angles) * inv_root, -jnp.sin(angles) * inv_root], axis=1).astype(
        jnp.bfloat16
    )


def band_energy(fourier, basis_block, orders):
    coefficients = jnp.einsum(
        "fpmbcn,nml->fpmbcl", fourier, basis_block, preferred_element_type=jnp.float32
    )
    squares = jnp.sum(coefficients * coefficients, axis=1)
    weights = jnp.where(orders == 0, 1.0, 2.0).astype(jnp.float32)
    return jnp.sum(squares * weights[None, :, None, None, None], axis=(1, 2))


def body(predicted, target, legendre_basis):
    groups = lax.axis_size("batch")
    band_count = lax.axis_size("lat")
    per_dev = legendre_basis.shape[1]
    order_count = per_dev * groups * band_count
    dft_table = fourier_table(predicted.shape[3], order_count)
    band_id = lax.axis_index("lat")

    def transform(field_in):
        return jnp.einsum(
            "bcnk,kpm->pmbcn", field_in, dft_table, preferred_element_type=jnp.float32
        ).astype(jnp.bfloat16)

    fourier = jnp.stack([transform(predicted), transform(target)], axis=0)
    members = fourier.shape[3]
    channels = fourier.shape[4]
    lat_rows = fourier.shape[5]
    fourier = fourier.reshape(2, 2, groups, band_count, per_dev, members, channels, lat_rows)
    arrived = lax.all_to_all(fourier, "lat", split_axis=3, concat_axis=7, tiled=True)
    arrived = arrived.reshape(
        2, 2, groups * per_dev, arrived.shape[5], arrived.shape[6], arrived.shape[7]
    )
    basis_block = lax.all_gather(legendre_basis, "batch", axis=1, tiled=True)
    taken = basis_block.shape[1]
    gathered_ids = jnp.arange(taken, dtype=jnp.int32)
    orders = (
        gathered_ids // per_dev * band_count * per_dev + band_id * per_dev + gathered_ids % per_dev
    )
    partial_value = band_energy(arrived, basis_block, orders)
    energy = lax.psum(partial_value, "lat")
    energy = lax.psum(energy, "batch")
    spectra = energy / (predicted.shape[0] * groups * order_count)
    log_spectra = jnp.log(spectra + 1e-06)
    channel_loss = jnp.mean((log_spectra[0] - log_spectra[1]) ** 2, axis=1)
    return (spectra, channel_loss)


def solution(mesh):
    placed = (
        P("batch", None, "lat", None),
        P("batch", None, "lat", None),
        P(None, ("batch", "lat"), None),
    )
    return jax.shard_map(body, mesh=mesh, in_specs=placed, out_specs=(P(), P()), check_vma=False)
```

profile of v0, /device:TPU:0, one launch (start us, length us, event | category | flops | bytes accessed | tf_op | source)
XLA Modules:
  0.0 212.2 jit_solution(11625327290755649896)
XLA Ops:
  7.2 0.0 all-gather.2.cloned.1.call-start
  7.2 0.7 all-gather.2.cloned.1.call-update
  7.9 2.6 %multiply_convert_fusion = (bf16[1440,1,96]{0,2,1:T(8,128)(2,1)S(1)}, bf16[1440,1,96]{0,2,1:T(8,128)(2,1)S(1)}) fusion(), kind=kLoop, calls=%fused_computation.17 | loop fusion | flops 1935360 | bytes 552960 | tf_op jit(solution)/shard_map/convert.1
  10.5 0.0 copy-start
  10.5 0.0 copy-start.1
  10.5 0.7 copy-done
  11.2 0.1 copy-done.1
  11.3 4.8 %fusion.8 = bf16[2,96,73,24]{1,2,3,0:T(8,128)(2,1)S(1)} fusion(bf16[73,24,1440]{2,1,0:T(8,128)(2,1)} %bitcast.33, bf16[1440,1,96]{0,2,1:T(8,128)(2,1)S(1)} %get-tuple-element.4, bf16[1440,1,96]{0,2,1:T(8,128)(2,1)S(1)} %get-tuple-element.5), kind=kOutput, calls=%fused_computation.11 | convolution fusion | flops 970228224 | bytes 6271488 | tf_op jit(solution)/shard_map/bcnk,kpm->pmbcn/dot_general | solution.py:37
  16.1 0.9 copy.29
  17.0 5.5 %fusion.11 = bf16[2,96,73,24]{1,2,3,0:T(8,128)(2,1)S(1)} fusion(bf16[73,24,1440]{2,1,0:T(8,128)(2,1)} %bitcast.34, bf16[1440,1,96]{0,2,1:T(8,128)(2,1)} %copy-done, bf16[1440,1,96]{0,2,1:T(8,128)(2,1)} %copy-done.1), kind=kOutput, calls=%fused_computation.12 | convolution fusion | flops 970228224 | bytes 6271488 | tf_op jit(solution)/shard_map/bcnk,kpm->pmbcn/dot_general | solution.py:37
  22.5 0.9 copy.31
  23.3 0.5 pad_maximum_fusion
  23.9 2.0 copy.32
  25.9 7.5 %all-to-all-start = ((bf16[2,2,4,8,3,1,73,24]{6,7,4,2,1,5,0,3:T(8,128)(2,1)}), bf16[2,2,4,8,3,1,73,24]{6,7,4,2,1,5,0,3:T(8,128)(2,1)S(1)}, u32[]{:S(2)}, u32[]{:S(2)}) async-start(bf16[2,2,4,8,3,1,73,24]{6,7,4,2,1,5,0,3:T(8,128)(2,1)} %copy.32), calls=%async_computation | async-start | bytes 4718592 | tf_op jit(solution)/shard_map/all_to_all | solution.py:46
  33.5 0.0 all-reduce.3.cloned.1.call-start
  33.5 53.6 %all-to-all-done = bf16[2,2,4,8,3,1,73,24]{6,7,4,2,1,5,0,3:T(8,128)(2,1)S(1)} async-done(((bf16[2,2,4,8,3,1,73,24]{6,7,4,2,1,5,0,3:T(8,128)(2,1)}), bf16[2,2,4,8,3,1,73,24]{6,7,4,2,1,5,0,3:T(8,128)(2,1)S(1)}, u32[]{:S(2)}, u32[]{:S(2)}) %all-to-all-start) | async-done | bytes 1345568 | tf_op jit(solution)/shard_map/all_to_all | solution.py:46
  87.1 2.1 copy.33
  89.2 0.0 all-gather.2.cloned.1.call-done
  89.2 5.1 %multiply_reduce_fusion = f32[12,2,73,720]{3,2,1,0:T(8,128)S(1)} fusion(bf16[192,12,720]{2,0,1:T(8,128)(2,1)} %all-gather.2.cloned.1.call-done, bf16[2,2,12,73,192]{3,4,2,1,0:T(8,128)(2,1)} %bitcast.30), kind=kOutput, calls=%fused_computation | convolution fusion | flops 972570240 | bytes 9709056 | tf_op jit(solution)/shard_map/fpmbcn,nml->fpmbcl/dot_general | solution.py:20
  94.3 0.6 multiply_reduce_fusion.1
  94.9 1.1 copy.40
  96.0 0.0 all-reduce.3.cloned.1.call-update
  96.1 0.0 all-reduce.5.cloned.1.call-start
  96.1 71.4 %all-reduce.3.cloned.1.call-done = f32[2,73,720]{2,0,1:T(2,128)} async-done(((f32[2,73,720]{2,0,1:T(2,128)}), f32[2,73,720]{2,0,1:T(2,128)}) %all-reduce.3.cloned.1.call-update) | async-done | bytes 420496 | tf_op jit(solution)/shard_map/psum | solution.py:57
  167.5 0.0 all-reduce.5.cloned.1.call-update
  167.6 34.7 %all-reduce.5.cloned.1.call-done = f32[2,73,720]{2,0,1:T(2,128)} async-done(((f32[2,73,720]{2,0,1:T(2,128)}), f32[2,73,720]{2,0,1:T(2,128)}) %all-reduce.5.cloned.1.call-update) | async-done | bytes 420496 | tf_op jit(solution)/shard_map/psum | solution.py:58
  202.2 2.2 %add_log_fusion = (f32[2,73,720]{2,0,1:T(2,128)S(1)}, f32[2,73,720]{2,0,1:T(2,128)}) fusion(f32[2,73,720]{2,0,1:T(2,128)} %all-reduce.5.cloned.1.call-done), kind=kLoop, calls=%fused_computation.23 | loop fusion | flops 210240 | bytes 1261440 | tf_op jit(solution)/shard_map/log | solution.py:60
  204.5 0.6 fusion.20
  205.1 0.5 broadcast_multiply_fusion.1
  (1 shorter events, 0.0 us)
Async XLA Ops:
  7.2 82.1 %all-gather.2.cloned.1.call-start = ((), (), s32[]{:S(2)}) async-start(), calls=%async_computation.1 | async-start | bytes 4423680 | tf_op jit(solution)/shard_map/all_gather | solution.py:50
  10.5 0.7 copy-start
  10.5 0.8 copy-start.1
  25.9 61.2 %all-to-all-start = ((bf16[2,2,4,8,3,1,73,24]{6,7,4,2,1,5,0,3:T(8,128)(2,1)}), bf16[2,2,4,8,3,1,73,24]{6,7,4,2,1,5,0,3:T(8,128)(2,1)S(1)}, u32[]{:S(2)}, u32[]{:S(2)}) async-start(bf16[2,2,4,8,3,1,73,24]{6,7,4,2,1,5,0,3:T(8,128)(2,1)} %copy.32), calls=%async_computation | async-start | bytes 4718592 | tf_op jit(solution)/shard_map/all_to_all | solution.py:46
  33.5 134.1 %all-reduce.3.cloned.1.call-start = ((), (), s32[]{:S(2)}) async-start(), calls=%async_computation.2 | async-start | bytes 897024 | tf_op jit(solution)/shard_map/psum | solution.py:57
  96.1 106.2 %all-reduce.5.cloned.1.call-start = ((), (), s32[]{:S(2)}) async-start(), calls=%async_computation.3 | async-start | bytes 897024 | tf_op jit(solution)/shard_map/psum | solution.py:58
Sparse Core Ops, SparseCore 0:
  9.5 33.4 all-gather.1
  96.2 71.2 all-reduce.2
  169.9 32.2 all-reduce.4
where the time goes:
time: 212 us
  waiting for transfers between devices  160 us (75%)
  matrix products  15.4 us (7%)
  between operations  13.8 us (7%)
  local copies, waits for them, and re-layouts  7.77 us (4%)
  starting transfers between devices  7.66 us (4%)
  other arithmetic  7.07 us (3%)
    psum x1, waiting for transfers between devices, body(): energy = lax.psum(partial_value, 'lat')  71.4 us
    all_to_all x1, waiting for transfers between devices, body(): lax.all_to_all(fourier, 'lat', split_axis=3, concat_axis=7, tiled=True)  53.6 us
    psum x1, waiting for transfers between devices, body(): energy = lax.psum(energy, 'batch')  34.7 us
    dot_general x2, matrix products, transform(): jnp.einsum('bcnk,kpm->pmbcn', field_in, dft_table, preferred_element_type...  10.3 us
    all_to_all x1, starting transfers between devices, body(): lax.all_to_all(fourier, 'lat', split_axis=3, concat_axis=7, tiled=True)  7.55 us
    dot_general x1, matrix products, band_energy(): jnp.einsum('fpmbcn,nml->fpmbcl', fourier, basis_block, preferred_element_...  5.1 us
  transfers between devices with their start and end apart: 4, of which 3 were waited for; matrix products, arithmetic and copies ran while one was open for 9% of the time, Pallas kernels for 0%

commit v1 on v0

--- a/solution.py
+++ b/solution.py
@@ -54,7 +54,7 @@
         gathered_ids // per_dev * band_count * per_dev + band_id * per_dev + gathered_ids % per_dev
     )
     partial_value = band_energy(arrived, basis_block, orders)
-    energy = lax.psum(partial_value, "lat")
+    energy = lax.all_gather(partial_value, axis_name="lat").sum(axis=0)
     energy = lax.psum(energy, "batch")
     spectra = energy / (predicted.shape[0] * groups * order_count)
     log_spectra = jnp.log(spectra + 1e-06)

time: 212 us -> 209 us (0.986)
  waiting for transfers between devices: 160 us -> 155 us
  other arithmetic: 7.07 us -> 9.42 us
    psum x1 -> x0, waiting for transfers between devices: 71.4 us -> none  [body(): energy = lax.psum(partial_value, 'lat')]
    all_gather x0 -> x1, waiting for transfers between devices: none -> 68.7 us  [body(): energy = lax.all_gather(partial_value, axis_name='lat').sum(axis=0)]
    reduce_sum x0 -> x1, other arithmetic: none -> 3.19 us  [body(): energy = lax.all_gather(partial_value, axis_name='lat').sum(axis=0)]
    psum x1, waiting for transfers between devices: 34.7 us -> 32.1 us  [body(): energy = lax.psum(energy, 'batch')]
where the time goes in v1:
time: 209 us
  waiting for transfers between devices  155 us (74%)
  matrix products  15.4 us (7%)
  between operations  13.8 us (7%)
  other arithmetic  9.42 us (5%)
  local copies, waits for them, and re-layouts  7.77 us (4%)
  starting transfers between devices  7.66 us (4%)
    all_gather x1, waiting for transfers between devices, body(): energy = lax.all_gather(partial_value, axis_name='lat').sum(axis=0)  68.7 us
    all_to_all x1, waiting for transfers between devices, body(): lax.all_to_all(fourier, 'lat', split_axis=3, concat_axis=7, tiled=True)  53.6 us
    psum x1, waiting for transfers between devices, body(): energy = lax.psum(energy, 'batch')  32.1 us
    dot_general x2, matrix products, transform(): jnp.einsum('bcnk,kpm->pmbcn', field_in, dft_table, preferred_element_type...  10.3 us
    all_to_all x1, starting transfers between devices, body(): lax.all_to_all(fourier, 'lat', split_axis=3, concat_axis=7, tiled=True)  7.55 us
    dot_general x1, matrix products, band_energy(): jnp.einsum('fpmbcn,nml->fpmbcl', fourier, basis_block, preferred_element_...  5.1 us
  transfers between devices with their start and end apart: 4, of which 3 were waited for; matrix products, arithmetic and copies ran while one was open for 9% of the time, Pallas kernels for 0%

profile of v1, /device:TPU:0, one launch (start us, length us, event | category | flops | bytes accessed | tf_op | source)
XLA Modules:
  0.0 209.2 jit_solution(16903829719918162033)
XLA Ops:
  7.2 0.0 all-gather.4.cloned.1.call-start
  7.2 0.7 all-gather.4.cloned.1.call-update
  7.9 2.6 %multiply_convert_fusion = (bf16[1440,1,96]{0,2,1:T(8,128)(2,1)S(1)}, bf16[1440,1,96]{0,2,1:T(8,128)(2,1)S(1)}) fusion(), kind=kLoop, calls=%fused_computation.17 | loop fusion | flops 1935360 | bytes 552960 | tf_op jit(solution)/shard_map/convert.1
  10.5 0.0 copy-start
  10.5 0.0 copy-start.1
  10.5 0.7 copy-done
  11.2 0.1 copy-done.1
  11.3 4.8 %fusion.8 = bf16[2,96,73,24]{1,2,3,0:T(8,128)(2,1)S(1)} fusion(bf16[73,24,1440]{2,1,0:T(8,128)(2,1)} %bitcast.35, bf16[1440,1,96]{0,2,1:T(8,128)(2,1)S(1)} %get-tuple-element.10, bf16[1440,1,96]{0,2,1:T(8,128)(2,1)S(1)} %get-tuple-element.11), kind=kOutput, calls=%fused_computation.11 | convolution fusion | flops 970228224 | bytes 6271488 | tf_op jit(solution)/shard_map/bcnk,kpm->pmbcn/dot_general | solution.py:37
  16.1 0.9 copy.39
  17.0 5.5 %fusion.11 = bf16[2,96,73,24]{1,2,3,0:T(8,128)(2,1)S(1)} fusion(bf16[73,24,1440]{2,1,0:T(8,128)(2,1)} %bitcast.36, bf16[1440,1,96]{0,2,1:T(8,128)(2,1)} %copy-done, bf16[1440,1,96]{0,2,1:T(8,128)(2,1)} %copy-done.1), kind=kOutput, calls=%fused_computation.12 | convolution fusion | flops 970228224 | bytes 6271488 | tf_op jit(solution)/shard_map/bcnk,kpm->pmbcn/dot_general | solution.py:37
  22.5 0.9 copy.41
  23.3 0.5 pad_maximum_fusion
  23.9 2.0 copy.42
  25.9 7.5 %all-to-all-start = ((bf16[2,2,4,8,3,1,73,24]{6,7,4,2,1,5,0,3:T(8,128)(2,1)}), bf16[2,2,4,8,3,1,73,24]{6,7,4,2,1,5,0,3:T(8,128)(2,1)S(1)}, u32[]{:S(2)}, u32[]{:S(2)}) async-start(bf16[2,2,4,8,3,1,73,24]{6,7,4,2,1,5,0,3:T(8,128)(2,1)} %copy.42), calls=%async_computation | async-start | bytes 4718592 | tf_op jit(solution)/shard_map/all_to_all | solution.py:46
  33.5 0.0 all-gather.6.cloned.1.call-start
  33.5 53.6 %all-to-all-done = bf16[2,2,4,8,3,1,73,24]{6,7,4,2,1,5,0,3:T(8,128)(2,1)S(1)} async-done(((bf16[2,2,4,8,3,1,73,24]{6,7,4,2,1,5,0,3:T(8,128)(2,1)}), bf16[2,2,4,8,3,1,73,24]{6,7,4,2,1,5,0,3:T(8,128)(2,1)S(1)}, u32[]{:S(2)}, u32[]{:S(2)}) %all-to-all-start) | async-done | bytes 1345568 | tf_op jit(solution)/shard_map/all_to_all | solution.py:46
  87.1 2.1 %copy.43 = bf16[2,2,4,1,3,1,73,8,24]{6,8,7,4,2,1,0,5,3:T(8,128)(2,1)} copy(bf16[2,2,4,1,3,1,73,8,24]{6,8,4,2,1,0,7,5,3:T(8,128)(2,1)S(1)} %bitcast.30) | data formatting | bytes 2691072 | tf_op jit(solution)/shard_map/all_to_all | solution.py:46
  89.2 0.0 all-gather.4.cloned.1.call-done
  89.2 5.1 %multiply_reduce_fusion = f32[12,2,73,720]{3,2,1,0:T(8,128)S(1)} fusion(bf16[192,12,720]{2,0,1:T(8,128)(2,1)} %all-gather.4.cloned.1.call-done, bf16[2,2,12,73,192]{3,4,2,1,0:T(8,128)(2,1)} %bitcast.31), kind=kOutput, calls=%fused_computation | convolution fusion | flops 972570240 | bytes 9709056 | tf_op jit(solution)/shard_map/fpmbcn,nml->fpmbcl/dot_general | solution.py:20
  94.3 1.3 multiply_reduce_fusion.1
  95.7 0.0 all-gather.6.cloned.1.call-update
  95.7 0.0 all-reduce.2.cloned.1.call-start
  95.8 68.7 %all-gather.6.cloned.1.call-done = f32[16,73,720]{2,1,0:T(8,128)} async-done(((f32[2,73,720]{2,1,0:T(8,128)}), f32[16,73,720]{2,1,0:T(8,128)}) %all-gather.6.cloned.1.call-update) | async-done | bytes 3363856 | tf_op jit(solution)/shard_map/all_gather | solution.py:57
  164.4 3.2 %reduce_sum.38 = f32[2,73,720]{2,1,0:T(8,128)} reduce(f32[8,2,73,720]{3,2,1,0:T(8,128)} %bitcast.34, f32[]{:T(128)} %constant.47.clone.1), dimensions={0}, to_apply=%region_2.3 | reduce | flops 735840 | bytes 3784324 | tf_op jit(solution)/shard_map/reduce_sum | solution.py:57
  167.6 0.0 all-reduce.2.cloned.1.call-update
  167.6 32.1 %all-reduce.2.cloned.1.call-done = f32[2,73,720]{2,1,0:T(8,128)} async-done(((f32[2,73,720]{2,1,0:T(8,128)}), f32[2,73,720]{2,1,0:T(8,128)}) %all-reduce.2.cloned.1.call-update) | async-done | bytes 420496 | tf_op jit(solution)/shard_map/psum | solution.py:58
  199.7 1.1 add_log_fusion
  200.9 1.1 copy.47
  202.0 0.1 fusion.20
  202.1 0.5 broadcast_multiply_fusion.1
  (1 shorter events, 0.0 us)
Async XLA Ops:
  7.2 82.1 %all-gather.4.cloned.1.call-start = ((), (), s32[]{:S(2)}) async-start(), calls=%async_computation.1 | async-start | bytes 4423680 | tf_op jit(solution)/shard_map/all_gather | solution.py:50
  10.5 0.7 copy-start
  10.5 0.8 copy-start.1
  25.9 61.2 %all-to-all-start = ((bf16[2,2,4,8,3,1,73,24]{6,7,4,2,1,5,0,3:T(8,128)(2,1)}), bf16[2,2,4,8,3,1,73,24]{6,7,4,2,1,5,0,3:T(8,128)(2,1)S(1)}, u32[]{:S(2)}, u32[]{:S(2)}) async-start(bf16[2,2,4,8,3,1,73,24]{6,7,4,2,1,5,0,3:T(8,128)(2,1)} %copy.42), calls=%async_computation | async-start | bytes 4718592 | tf_op jit(solution)/shard_map/all_to_all | solution.py:46
  33.5 131.0 %all-gather.6.cloned.1.call-start = ((), (), s32[]{:S(2)}) async-start(), calls=%async_computation.3 | async-start | bytes 4423680 | tf_op jit(solution)/shard_map/all_gather | solution.py:57
  95.7 104.0 %all-reduce.2.cloned.1.call-start = ((), (), s32[]{:S(2)}) async-start(), calls=%async_computation.2 | async-start | bytes 983040 | tf_op jit(solution)/shard_map/psum | solution.py:58
Sparse Core Ops, SparseCore 0:
  9.5 33.4 all-gather.3
  95.8 68.5 all-gather.5
  167.8 31.9 all-reduce.1
